TPU v7x, 32 devices: a whole 2x2x4 slice. The times are simulated.
32 devices in a mesh: grow: 8 (over y, x, core), gcol: 4 (over z).
Axes of the slice: x: 2, y: 2, z: 4, core: 2. Of those that a mesh axis runs over, the one named last changes fastest.
Arguments:
- eps_static: float32 [12288, 12288], P('grow', 'gcol'), may hold values from -1.8 to 1.8
- eps_imag: float32 [12288, 12288], P('grow', 'gcol'), may hold values from -1.8 to 1.8
- frequency_grid: float32 [3], replicated, may hold values from 0.1 to 2
- band_energy: float32 [32], replicated, may hold values from -2 to 2
- pair_elements: bfloat16 [32, 64, 12288], P('grow', None, 'gcol'), may hold values from -0.0546875 to 0.0546875
Outputs:
- sigma: float32 [3, 64], P(None, 'gcol')
All inputs are finite; a program needn't handle non-finite values.
Results may differ from a plain program's by a relative error of at most 0.0019.
Values may be sent and summed in bfloat16 or wider, within the bound.
A program may use at most 128 MiB of HBM per device.

v0:
```python
import jax
import jax.numpy as jnp
from jax import lax
from jax.sharding import PartitionSpec as P

NE = 3


def broadcast(block, axis, owner):
    block = jnp.where(lax.axis_index(axis) == owner, block, jnp.zeros_like(block))
    return lax.psum(block, axis)


def shards(eps_static, eps_imag, frequency_grid, band_energy, pair_elements):
    row_count = lax.axis_size("grow")
    col_count = lax.axis_size("gcol")
    group_ratio = row_count // col_count
    row_index = lax.axis_index("grow")
    col_index = lax.axis_index("gcol")
    height = eps_static.shape[0]
    breadth = eps_static.shape[1]
    bands = pair_elements.shape[0] * row_count
    states = pair_elements.shape[1]
    column_panel = lax.all_gather(pair_elements, "grow", axis=0, tiled=True)
    offset = row_index % group_ratio * height
    section = lax.dynamic_slice_in_dim(column_panel, offset, height, 2)
    row_panel = broadcast(section, "gcol", row_index // group_ratio)
    global_rows = row_index * height + lax.iota(jnp.int32, height)
    global_cols = col_index * breadth + lax.iota(jnp.int32, breadth)
    kronecker = (global_rows[:, None] == global_cols[None, :]).astype(jnp.float32)
    static_part = eps_static - kronecker
    imag_part = eps_imag - kronecker
    spread = static_part - imag_part
    pole_square = (imag_part * imag_part + 0.25) / (spread * spread + 0.25)
    pole_freq = jnp.sqrt(pole_square)
    strength = -static_part * pole_square
    left_rows = row_panel.reshape(bands * states, height)
    right_rows = column_panel.reshape(bands * states, breadth)
    terms = []
    for point in range(NE):
        kernel = (strength / (pole_freq * (pole_freq + frequency_grid[point]))).astype(jnp.bfloat16)
        projected = jnp.dot(left_rows, kernel, preferred_element_type=jnp.float32)
        terms.append(jnp.sum(projected * right_rows, axis=1))
    quad = jnp.stack(terms).reshape(NE, bands, states)
    offset_energy = frequency_grid[:, None] - band_energy[None, :]
    weight = 1.0 / (1.0 + offset_energy * offset_energy)
    partial_sigma = jnp.einsum("em,ems->es", weight, quad)
    shares = lax.psum_scatter(partial_sigma, "gcol", scatter_dimension=1, tiled=True)
    return lax.psum(shares, "grow")


def solution(mesh):
    return jax.shard_map(
        shards,
        mesh=mesh,
        in_specs=(P("grow", "gcol"), P("grow", "gcol"), P(), P(), P("grow", None, "gcol")),
        out_specs=P(None, "gcol"),
        check_vma=False,
    )
```

profile of v0, /device:TPU:0, one launch (start us, length us, event | category | flops | bytes accessed | tf_op | source)
XLA Modules:
  0.0 466.5 jit_solution(14416005977616240631)
XLA Ops:
  6.5 0.0 copy-start.1
  6.5 0.0 copy-start.3
  6.5 0.0 all-gather.2.cloned.1.call-start
  6.5 0.7 all-gather.2.cloned.1.call-update
  7.3 0.0 all-reduce.2.cloned.1.call-start
  7.3 76.6 %all-gather.2.cloned.1.call-done = bf16[32,64,3072]{2,1,0:T(8,128)(2,1)} async-done(((bf16[4,64,3072]{2,1,0:T(8,128)(2,1)}), bf16[32,64,3072]{2,1,0:T(8,128)(2,1)}) %all-gather.2.cloned.1.call-update) | async-done | bytes 12582928 | tf_op jit(solution)/shard_map/all_gather | solution.py:24
  84.0 6.9 %dynamic-slice_select_fusion = bf16[32,64,1536]{2,1,0:T(8,128)(2,1)} fusion(bf16[32,64,3072]{2,1,0:T(8,128)(2,1)} %all-gather.2.cloned.1.call-done, s32[]{:T(128)S(6)} %select_n.25, pred[]{:T(512)S(6)} %eq.18), kind=kLoop, calls=%fused_computation.19 | loop fusion | flops 3145728 | bytes 12582917 | tf_op jit(solution)/shard_map/jit(_where)/select_n | solution.py:10
  90.9 0.0 all-reduce.2.cloned.1.call-update
  90.9 0.0 reduce-scatter.4.cloned.1.call-start
  90.9 0.0 copy-done.1
  91.0 0.6 fusion.20
  91.6 0.0 copy-done.3
  91.6 0.6 divide_bitcast_fusion
  92.2 221.7 %all-reduce.2.cloned.1.call-done = bf16[2048,1536]{1,0:T(8,128)(2,1)} async-done(((bf16[2048,1536]{1,0:T(8,128)(2,1)}), bf16[2048,1536]{1,0:T(8,128)(2,1)}) %all-reduce.2.cloned.1.call-update) | async-done | bytes 6291472 | tf_op jit(solution)/shard_map/psum | solution.py:11
  313.9 37.5 %fusion = bf16[2048]{0:T(1024)(128)(2,1)S(1)} fusion(bf16[2048,3072]{1,0:T(8,128)(2,1)} %bitcast.17, bf16[2048,1536]{1,0:T(8,128)(2,1)} %all-reduce.2.cloned.1.call-done, f32[]{:T(128)} %bitcast.2, f32[1536,3072]{1,0:T(8,128)} %param.5, s32[3072]{0:T(1024)S(1)} %iota_add_fusion, s32[1536]{0:T(1024)S(1)} %iota_add_fusion.1, f32[1536,3072]{1,0:T(8,128)} %param.6), kind=kOutput, calls=%fused_computation.8 | convolution fusion | flops 19421722624 | bytes 56645636 | tf_op jit(solution)/shard_map/dot_general | solution.py:42
  351.4 0.7 stack.12
  352.1 37.6 %fusion.1 = bf16[2048]{0:T(1024)(128)(2,1)S(1)} fusion(bf16[2048,3072]{1,0:T(8,128)(2,1)} %bitcast.18, bf16[2048,1536]{1,0:T(8,128)(2,1)} %all-reduce.2.cloned.1.call-done, f32[]{:T(128)} %bitcast.4, f32[1536,3072]{1,0:T(8,128)} %param.5, s32[3072]{0:T(1024)S(1)} %iota_add_fusion, s32[1536]{0:T(1024)S(1)} %iota_add_fusion.1, f32[1536,3072]{1,0:T(8,128)} %param.6), kind=kOutput, calls=%fused_computation.9 | convolution fusion | flops 19421722624 | bytes 56645636 | tf_op jit(solution)/shard_map/dot_general | solution.py:42
  389.7 0.1 stack.13
  389.8 0.0 copy-start
  389.8 0.0 copy-start.2
  389.8 37.7 %fusion.2 = bf16[2048]{0:T(1024)(128)(2,1)S(1)} fusion(bf16[2048,3072]{1,0:T(8,128)(2,1)} %bitcast.19, bf16[2048,1536]{1,0:T(8,128)(2,1)} %all-reduce.2.cloned.1.call-done, f32[]{:T(128)} %bitcast.6, f32[1536,3072]{1,0:T(8,128)} %param.5, s32[3072]{0:T(1024)S(1)} %iota_add_fusion, s32[1536]{0:T(1024)S(1)} %iota_add_fusion.1, f32[1536,3072]{1,0:T(8,128)} %param.6), kind=kOutput, calls=%fused_computation.10 | convolution fusion | flops 19421722624 | bytes 56645636 | tf_op jit(solution)/shard_map/dot_general | solution.py:42
  427.5 0.1 stack.14
  427.6 0.0 copy-done
  427.6 0.0 copy-done.2
  427.6 0.1 fusion.12
  427.8 0.7 copy.8
  428.5 0.0 reduce-scatter.4.cloned.1.call-update
  428.5 18.3 %reduce-scatter.4.cloned.1.call-done = f32[16,3]{1,0:T(8,128)} async-done(((f32[64,3]{1,0:T(8,128)}), f32[16,3]{1,0:T(8,128)}) %reduce-scatter.4.cloned.1.call-update) | async-done | bytes 208
  446.8 0.8 copy.9
  447.6 12.4 %psum.15 = f32[3,16]{1,0:T(4,128)} all-reduce(f32[3,16]{1,0:T(4,128)S(1)} %copy.9), channel_id=1, replica_groups=mesh['grow'=8,'gcol'=4] {'grow'}, use_global_device_ids=true, to_apply=%region_5.6 | all-reduce | flops 48 | bytes 384 | tf_op jit(solution)/shard_map/psum | solution.py:49
  (3 shorter events, 0.0 us)
Async XLA Ops:
  6.5 84.4 %copy-start.1 = (f32[3]{0:T(128)S(1)}, f32[3]{0:T(128)}, u32[]{:S(2)}) copy-start(f32[3]{0:T(128)} %param.7) | copy-start | bytes 40
  6.5 85.0 %copy-start.3 = (f32[32]{0:T(128)S(1)}, f32[32]{0:T(128)}, u32[]{:S(2)}) copy-start(f32[32]{0:T(128)} %param.8) | copy-start | bytes 388
  6.5 77.4 %all-gather.2.cloned.1.call-start = ((), (), s32[]{:S(2)}) async-start(), calls=%async_computation.1 | async-start | bytes 14155776 | tf_op jit(solution)/shard_map/all_gather | solution.py:24
  7.3 306.6 %all-reduce.2.cloned.1.call-start = ((), (), s32[]{:S(2)}) async-start(), calls=%async_computation.2 | async-start | bytes 12582912 | tf_op jit(solution)/shard_map/psum | solution.py:11
  90.9 355.9 %reduce-scatter.4.cloned.1.call-start = ((), (), s32[]{:S(2)}) async-start(), calls=%async_computation.3 | async-start | bytes 40960
  389.8 37.8 %copy-start = (bf16[1,32,64]{2,1,0:T(8,128)(2,1)S(1)}, bf16[1,32,64]{2,1,0:T(8,128)(2,1)}, u32[]{:S(2)}) copy-start(bf16[1,32,64]{2,1,0:T(8,128)(2,1)} %stack.12) | copy-start | bytes 12292
  389.8 37.8 %copy-start.2 = (bf16[3,32,1]{1,0,2:T(4,128)(2,1)S(1)}, bf16[3,32,1]{1,0,2:T(4,128)(2,1)}, u32[]{:S(2)}) copy-start(bf16[3,32,1]{1,0,2:T(4,128)(2,1)} %divide_bitcast_fusion) | copy-start | bytes 580
Sparse Core Ops, SparseCore 0:
  9.2 74.7 all-gather.1
  91.0 222.8 all-reduce.1
  428.6 18.1 reduce-scatter.3
where the time goes:
time: 467 us; the launch traced here: 466 us
  waiting for transfers between devices  317 us (68%)
  matrix products  113 us (24%)
  between operations  13.2 us (3%)
  blocking collectives  12.4 us (3%)
  other arithmetic  7.55 us (2%)
    psum x1, waiting for transfers between devices, broadcast(): return lax.psum(block, axis)  222 us
    dot_general x3, matrix products, shards(): projected = jnp.dot(left_rows, kernel, preferred_element_type=jnp.float32)  113 us
    all_gather x1, waiting for transfers between devices, shards(): column_panel = lax.all_gather(pair_elements, 'grow', axis=0, tiled=True)  76.6 us
    unnamed x4, waiting for transfers between devices  19 us
    psum x1, blocking collectives, shards(): return lax.psum(shares, 'grow')  12.4 us
  transfers between devices with their start and end apart: 3, of which 3 were waited for; matrix products, arithmetic and copies ran while one was open for 0% of the time, Pallas kernels for 0%

commit v1 on v0

v1 whole, which is shorter than its diff:
```python
import functools

import jax
import jax.numpy as jnp
from jax import lax
from jax.experimental import pallas as pl
from jax.experimental.pallas import tpu as pltpu
from jax.sharding import PartitionSpec as P

LANES = 128
SUB_ROWS = 32
SUB_COLS = 512
DOT_COLS = 256


def bit_flip(index, mask, extent):
    total, bit = 0, 1
    while bit < extent:
        total = total + ((index // bit + mask // bit) % 2) * bit
        bit *= 2
    return total


def body(R, Z, bpd, states, height, breadth, ne,
         freq, energy, es_hbm, ei_hbm, pair_hbm, out,
         kern, colp, rowp, es_buf, ei_buf, sig, part, recv1, recv2,
         eps_sem, own_sem, col_send, col_recv, row_recv, up_send, dn_send,
         s1_send, s1_recv, s2_send, s2_recv):
    r = lax.axis_index("grow")
    z = lax.axis_index("gcol")
    ratio = R // Z
    home = r // ratio
    offset = pl.multiple_of(r % ratio * height, height)
    spc = states // Z
    units = R * bpd
    blocks = 4 * bpd
    rows = height // blocks

    def dev(row, col):
        return dict(device_id={"grow": row, "gcol": col}, device_id_type=pl.DeviceIdType.MESH)

    def eps_copies(block, slot):
        at = pl.multiple_of(block * rows, rows)
        return (pltpu.make_async_copy(es_hbm.at[pl.ds(at, rows), :], es_buf.at[slot], eps_sem.at[0, slot]),
                pltpu.make_async_copy(ei_hbm.at[pl.ds(at, rows), :], ei_buf.at[slot], eps_sem.at[1, slot]))

    own = pltpu.make_async_copy(pair_hbm, colp.at[0], own_sem)
    own.start()
    for copy in eps_copies(0, 0):
        copy.start()

    barrier = pltpu.get_barrier_semaphore()
    for d in range(1, R):
        pl.semaphore_signal(barrier, inc=1, **dev((r + d) % R, z))
    for d in range(1, Z):
        pl.semaphore_signal(barrier, inc=1, **dev(r, (z + d) % Z))
    sig[...] = jnp.zeros_like(sig)
    own.wait()
    pl.semaphore_wait(barrier, R + Z - 2)

    def unit_rows(b):
        return pl.ds(pl.multiple_of(b * states, states), states)

    def col_copy(src_shard, dst_shard, b, row):
        return pltpu.make_async_remote_copy(
            src_ref=colp.at[src_shard, unit_rows(b), :], dst_ref=colp.at[dst_shard, unit_rows(b), :],
            send_sem=col_send.at[dst_shard * bpd + b], recv_sem=col_recv.at[dst_shard * bpd + b],
            **dev(row, z))

    partner = bit_flip(r, 1, R)

    def send_own(b, carry):
        col_copy(0, 1, b, partner).start()
        return carry
    lax.fori_loop(0, bpd, send_own, 0)
    for shard in range(2, R, 2):
        peer = bit_flip(r, shard, R)

        def send_far(b, carry, shard=shard, peer=peer):
            col_copy(0, shard, b, peer).start()
            return carry
        lax.fori_loop(0, bpd, send_far, 0)

    def row_copy(shard, b, u, sems, col):
        ref = rowp.at[shard, unit_rows(b), :]
        return pltpu.make_async_remote_copy(
            src_ref=ref, dst_ref=ref, send_sem=sems.at[u], recv_sem=row_recv.at[u], **dev(r, col))

    goes_up = jnp.logical_and(z >= home, z < Z - 1)
    goes_down = jnp.logical_and(z <= home, z > 0)
    upper = (z + 1) % Z
    lower = (z + Z - 1) % Z

    def comm(u):
        shard, b = u // bpd, u % bpd

        @pl.when(shard >= 1)
        def _():
            col_copy(0, shard, b, partner).wait_recv()

        @pl.when(jnp.logical_and(shard >= 2, shard % 2 == 0))
        def _():
            col_copy(shard, shard + 1, b, partner).start()

        @pl.when(z == home)
        def _():
            local = pltpu.make_async_copy(
                colp.at[shard, unit_rows(b), pl.ds(offset, height)],
                rowp.at[shard, unit_rows(b), :], row_recv.at[u])
            local.start()
            local.wait()

        @pl.when(z != home)
        def _():
            row_copy(shard, b, u, up_send, upper).wait_recv()

        @pl.when(goes_up)
        def _():
            row_copy(shard, b, u, up_send, upper).start()

        @pl.when(goes_down)
        def _():
            row_copy(shard, b, u, dn_send, lower).start()

    diagonal = r * height - z * breadth
    sub_rows = min(SUB_ROWS, rows)
    sub_cols = min(SUB_COLS, breadth)
    col_steps = breadth // sub_cols
    f0, f1, f2 = freq[0], freq[1], freq[2]

    def make_block(block):
        slot = block % 2

        @pl.when(block + 1 < blocks)
        def _():
            for copy in eps_copies(block + 1, 1 - slot):
                copy.start()
        for copy in eps_copies(block, slot):
            copy.wait()
        base = pl.multiple_of(block * rows, rows)

        def chunk(n, carry):
            at_row = pl.multiple_of(n // col_steps * sub_rows, sub_rows)
            at_col = pl.multiple_of(n % col_steps * sub_cols, sub_cols)
            where = (pl.ds(at_row, sub_rows), pl.ds(at_col, sub_cols))
            gap = (lax.broadcasted_iota(jnp.int32, (sub_rows, sub_cols), 0)
                   - lax.broadcasted_iota(jnp.int32, (sub_rows, sub_cols), 1))
            one = jnp.where(gap == at_col - at_row - base - diagonal, 1.0, 0.0)
            static = es_buf[(slot,) + where] - one
            imag = ei_buf[(slot,) + where] - one
            spread = static - imag
            over = imag * imag + 0.25
            under = spread * spread + 0.25
            pole = over * lax.rsqrt(over * under)
            p0, p1, p2 = pole + f0, pole + f1, pole + f2
            p01 = p0 * p1
            scale = -static * pole / (p01 * p2)
            to = (pl.ds(pl.multiple_of(base + at_row, sub_rows), sub_rows), where[1])
            kern[(0,) + to] = (p1 * p2 * scale).astype(jnp.bfloat16)
            kern[(1,) + to] = (p0 * p2 * scale).astype(jnp.bfloat16)
            kern[(2,) + to] = (p01 * scale).astype(jnp.bfloat16)
            return carry
        lax.fori_loop(0, rows // sub_rows * col_steps, chunk, 0)

    width = breadth // bpd
    dot_cols = min(DOT_COLS, width)
    while width % dot_cols:
        dot_cols //= 2

    def piece(number):
        shard, q = number // bpd, number % bpd
        first = bit_flip(r, shard, R) * bpd

        def step(n, carry):
            cols = pl.ds(pl.multiple_of(q * width + n * dot_cols, dot_cols), dot_cols)
            right = colp[shard, :, cols].astype(jnp.float32)
            left = rowp[shard]
            sums = []
            for e in range(ne):
                prod = jnp.dot(left, kern[e, :, cols], preferred_element_type=jnp.float32) * right
                thin = prod[:, :LANES]
                for k in range(1, dot_cols // LANES):
                    thin = thin + prod[:, k * LANES:(k + 1) * LANES]
                total = carry[e]
                for b in range(bpd):
                    miss = jnp.full((8, LANES), freq[e] - energy[first + b], jnp.float32)
                    weight = (1.0 / (1.0 + miss * miss))[:1]
                    total = total + weight * thin[b * states:(b + 1) * states]
                sums.append(total)
            return tuple(sums)
        start = tuple(sig[e] for e in range(ne))
        done = lax.fori_loop(0, width // dot_cols, step, start)
        for e in range(ne):
            sig[e] = done[e]

    def phase_a(u, carry):
        comm(u)
        make_block(2 * u)
        make_block(2 * u + 1)
        return carry
    lax.fori_loop(0, 2 * bpd, phase_a, 0)

    def phase_b(u, carry):
        comm(u)
        piece(2 * (u - 2 * bpd))
        piece(2 * (u - 2 * bpd) + 1)
        return carry
    lax.fori_loop(2 * bpd, 3 * bpd, phase_b, 0)

    def phase_c(u, carry):
        comm(u)
        piece(u - bpd)
        return carry
    lax.fori_loop(3 * bpd, units, phase_c, 0)

    def phase_d(u, carry):
        piece(u - bpd)
        return carry
    lax.fori_loop(units, units + bpd, phase_d, 0)

    for owner in range(Z):
        for e in range(ne):
            part[owner, e] = sig[e, owner * spc:(owner + 1) * spc]

    def s1_copy(d):
        return pltpu.make_async_remote_copy(
            src_ref=part.at[(z + d) % Z], dst_ref=recv1.at[d - 1],
            send_sem=s1_send.at[d - 1], recv_sem=s1_recv.at[d - 1], **dev(r, (z + d) % Z))

    def s2_copy(d, owner):
        return pltpu.make_async_remote_copy(
            src_ref=recv2.at[owner], dst_ref=recv2.at[owner],
            send_sem=s2_send.at[d - 1], recv_sem=s2_recv.at[owner], **dev((r + d) % R, z))

    for d in range(1, Z):
        s1_copy(d).start()

    def drain(u, carry):
        shard, b = u // bpd, u % bpd

        @pl.when(shard >= 1)
        def _():
            col_copy(0, shard, b, partner).wait_send()

        @pl.when(goes_up)
        def _():
            row_copy(shard, b, u, up_send, upper).wait_send()

        @pl.when(goes_down)
        def _():
            row_copy(shard, b, u, dn_send, lower).wait_send()
        return carry
    lax.fori_loop(0, units, drain, 0)

    mine = part[z]
    for d in range(1, Z):
        s1_copy(d).wait_recv()
        mine = mine + recv1[d - 1]
    recv2[r] = mine
    for d in range(1, R):
        s2_copy(d, r).start()
    for d in range(1, R):
        s2_copy(d, (r + R - d) % R).wait_recv()
    full = recv2[0]
    for owner in range(1, R):
        full = full + recv2[owner]
    out[...] = jnp.sum(full, axis=-1)
    for d in range(1, Z):
        s1_copy(d).wait_send()
    for d in range(1, R):
        s2_copy(d, r).wait_send()


def solution(mesh):
    R, Z = mesh.shape["grow"], mesh.shape["gcol"]

    def shards(eps_static, eps_imag, frequency_grid, band_energy, pair_elements):
        height, breadth = eps_static.shape
        bpd, states, _ = pair_elements.shape
        ne = frequency_grid.shape[0]
        spc = states // Z
        rows = height // (4 * bpd)
        dma = pltpu.SemaphoreType.DMA
        units = R * bpd
        any_space = pl.BlockSpec(memory_space=pl.ANY)
        smem = pl.BlockSpec(memory_space=pltpu.SMEM)
        return pl.pallas_call(
            functools.partial(body, R, Z, bpd, states, height, breadth, ne),
            out_shape=jax.ShapeDtypeStruct((ne, spc), jnp.float32),
            in_specs=[smem, smem, any_space, any_space, any_space],
            out_specs=pl.BlockSpec(memory_space=pltpu.VMEM),
            scratch_shapes=[
                pltpu.VMEM((ne, height, breadth), jnp.bfloat16),
                pltpu.VMEM((R, bpd * states, breadth), jnp.bfloat16),
                pltpu.VMEM((R, bpd * states, height), jnp.bfloat16),
                pltpu.VMEM((2, rows, breadth), jnp.float32),
                pltpu.VMEM((2, rows, breadth), jnp.float32),
                pltpu.VMEM((ne, states, LANES), jnp.float32),
                pltpu.VMEM((Z, ne, spc, LANES), jnp.float32),
                pltpu.VMEM((max(Z - 1, 1), ne, spc, LANES), jnp.float32),
                pltpu.VMEM((R, ne, spc, LANES), jnp.float32),
                dma((2, 2)), dma, dma((units,)), dma((units,)), dma((units,)),
                dma((units,)), dma((units,)),
                dma((Z,)), dma((Z,)), dma((R,)), dma((R,)),
            ],
            compiler_params=pltpu.CompilerParams(
                collective_id=0, has_side_effects=True, vmem_limit_bytes=62 * 1024 * 1024),
            name="pole_sigma",
        )(frequency_grid, band_energy, eps_static, eps_imag,
          pair_elements.reshape(bpd * states, breadth))

    return jax.shard_map(
        shards,
        mesh=mesh,
        in_specs=(P("grow", "gcol"), P("grow", "gcol"), P(), P(), P("grow", None, "gcol")),
        out_specs=P(None, "gcol"),
        check_vma=False,
    )
```

time: 467 us -> 181 us (0.39)
  waiting for transfers between devices: 317 us -> 0 us
  Pallas kernels: 0 us -> 179 us
  matrix products: 113 us -> 0 us
  between operations: 13.2 us -> 0.01 us
  blocking collectives: 12.4 us -> 0 us
  other arithmetic: 7.55 us -> 0 us
    psum x1 -> x0, waiting for transfers between devices: 222 us -> none  [broadcast(): return lax.psum(block, axis)]
    pallas_call x0 -> x1, Pallas kernels: none -> 179 us  [shards(): pl.pallas_call(functools.partial(body, R, Z, bpd, states, height, breadth...]
    dot_general x4 -> x0, matrix products: 113 us -> none  [the longest x3 113 us: shards(): projected = jnp.dot(left_rows, kernel, preferred_element_type=jnp.float32)]
    all_gather x1 -> x0, waiting for transfers between devices: 76.6 us -> none  [shards(): column_panel = lax.all_gather(pair_elements, 'grow', axis=0, tiled=True)]
    unnamed x4 -> x0, waiting for transfers between devices: 19 us -> none
    psum x1 -> x0, blocking collectives: 12.4 us -> none  [shards(): return lax.psum(shares, 'grow')]
    select_n x1 -> x0, other arithmetic: 6.9 us -> none  [broadcast(): jnp.where(lax.axis_index(axis) == owner, block, jnp.zeros_like(block))]
  transfers between devices with their start and end apart: 3 -> 0, of which waited for: 3 -> 0; matrix products, arithmetic and copies ran while one was open for 0% -> 0% of each run, Pallas kernels for 0% -> 0%
where the time goes in v1:
time: 181 us; the launch traced here: 180 us
  Pallas kernels  179 us (99%)
    pallas_call x1, Pallas kernels, shards(): pl.pallas_call(functools.partial(body, R, Z, bpd, states, height, breadth...  179 us

profile of v1, /device:TPU:0, one launch (start us, length us, event | category | flops | bytes accessed | tf_op | source)
XLA Modules:
  0.0 180.1 jit_solution(17567918647929016995)
XLA Ops:
  0.0 178.8 %pole_sigma.1 = f32[3,16]{1,0:T(4,128)} custom-call(f32[3]{0:T(128)} %freq.1, f32[32]{0:T(128)} %energy.1, f32[1536,3072]{1,0:T(8,128)} %es_hbm.1, f32[1536,3072]{1,0:T(8,128)} %ei_hbm.1, bf16[256,3072]{1,0:T(8,128)(2,1)} %bitcast.1), custom_call_target="tpu_custom_call" | custom-call | tf_op jit(solution)/shard_map/pole_sigma/pallas_call | solution.py:287
  178.8 1.3 copy.7

commit v2 on v1

--- a/solution.py
+++ b/solution.py
@@ -23,9 +23,9 @@
 
 def body(R, Z, bpd, states, height, breadth, ne,
          freq, energy, es_hbm, ei_hbm, pair_hbm, out,
-         kern, colp, rowp, es_buf, ei_buf, sig, part, recv1, recv2,
+         kern, colp, rowp, es_buf, ei_buf, sig, part, recv1, recv2, hold,
          eps_sem, own_sem, col_send, col_recv, row_recv, up_send, dn_send,
-         s1_send, s1_recv, s2_send, s2_recv):
+         s1_send, s1_recv, s2_send, s2_recv, hold_send, hold_recv, give_send):
     r = lax.axis_index("grow")
     z = lax.axis_index("gcol")
     ratio = R // Z
@@ -86,6 +86,67 @@
         return pltpu.make_async_remote_copy(
             src_ref=ref, dst_ref=ref, send_sem=sems.at[u], recv_sem=row_recv.at[u], **dev(r, col))
 
+    side = bpd // 2
+    keep = bpd - side
+    items = (Z - 1) * side
+    stride = 2 if 3 + 2 * (items - 1) < units else 1
+    relay_down = home == 0
+    relays = jnp.logical_or(relay_down, home == Z - 1)
+    ahead = jnp.where(relay_down, z - 1, z + 1)
+    has_ahead = jnp.logical_and(relays, jnp.logical_and(ahead >= 0, ahead < Z))
+    ahead_col = (ahead + Z) % Z
+
+    def side_copy(d, b):
+        dst = hold.at[d, unit_rows(b), :]
+        src = hold.at[d - 1, unit_rows(b), :] if not (isinstance(d, int) and d == 0) else colp.at[0, unit_rows(keep + b), :]
+        return pltpu.make_async_remote_copy(
+            src_ref=src, dst_ref=dst, send_sem=hold_send.at[d * side + b],
+            recv_sem=hold_recv.at[d * side + b], **dev(r, ahead_col))
+
+    def give_copy(d, b, k, panel):
+        to = panel * ratio + k
+        shard = bit_flip(r, to, R)
+        return pltpu.make_async_remote_copy(
+            src_ref=hold.at[d - 1, unit_rows(b), pl.ds(k * height, height)],
+            dst_ref=rowp.at[shard, unit_rows(keep + b), :],
+            send_sem=give_send.at[((d - 1) * side + b) * ratio + k],
+            recv_sem=row_recv.at[shard * bpd + keep + b], **dev(to, z))
+
+    def relay_item(t, act):
+        d, b = t // side + 1, t % side
+        panel = jnp.where(relay_down, z + d, z - d)
+
+        @pl.when(jnp.logical_and(relays, jnp.logical_and(panel >= 0, panel < Z)))
+        def _():
+            act(d, b, (panel + Z) % Z)
+
+    def pass_on(d, b, panel):
+        pltpu.make_async_remote_copy(
+            src_ref=hold.at[d - 1, unit_rows(b), :], dst_ref=hold.at[d - 1, unit_rows(b), :],
+            send_sem=hold_send.at[(d - 1) * side + b], recv_sem=hold_recv.at[(d - 1) * side + b],
+            **dev(r, ahead_col)).wait_recv()
+
+        @pl.when(has_ahead)
+        def _():
+            side_copy(d, b).start()
+        for k in range(ratio):
+            give_copy(d, b, k, panel).start()
+
+    def settle(d, b, panel):
+        @pl.when(has_ahead)
+        def _():
+            side_copy(d, b).wait_send()
+        for k in range(ratio):
+            give_copy(d, b, k, panel).wait_send()
+
+    @pl.when(has_ahead)
+    def _():
+        for b in range(side):
+            side_copy(0, b).start()
+
+    def aside(shard, b, group):
+        return jnp.logical_and(b >= keep, bit_flip(r, shard, R) // ratio == group)
+
     goes_up = jnp.logical_and(z >= home, z < Z - 1)
     goes_down = jnp.logical_and(z <= home, z > 0)
     upper = (z + 1) % Z
@@ -114,13 +175,18 @@
         def _():
             row_copy(shard, b, u, up_send, upper).wait_recv()
 
-        @pl.when(goes_up)
+        @pl.when(jnp.logical_and(goes_up, jnp.logical_not(aside(shard, b, Z - 1))))
         def _():
             row_copy(shard, b, u, up_send, upper).start()
 
-        @pl.when(goes_down)
+        @pl.when(jnp.logical_and(goes_down, jnp.logical_not(aside(shard, b, 0))))
         def _():
             row_copy(shard, b, u, dn_send, lower).start()
+
+        @pl.when(jnp.logical_and(jnp.logical_and(u >= 3, (u - 3) % stride == 0),
+                                 (u - 3) // stride < items))
+        def _():
+            relay_item((u - 3) // stride, pass_on)
 
     diagonal = r * height - z * breadth
     sub_rows = min(SUB_ROWS, rows)
@@ -242,15 +308,25 @@
         def _():
             col_copy(0, shard, b, partner).wait_send()
 
-        @pl.when(goes_up)
+        @pl.when(jnp.logical_and(goes_up, jnp.logical_not(aside(shard, b, Z - 1))))
         def _():
             row_copy(shard, b, u, up_send, upper).wait_send()
 
-        @pl.when(goes_down)
+        @pl.when(jnp.logical_and(goes_down, jnp.logical_not(aside(shard, b, 0))))
         def _():
             row_copy(shard, b, u, dn_send, lower).wait_send()
         return carry
     lax.fori_loop(0, units, drain, 0)
+
+    @pl.when(has_ahead)
+    def _():
+        for b in range(side):
+            side_copy(0, b).wait_send()
+
+    def drain_side(t, carry):
+        relay_item(t, settle)
+        return carry
+    lax.fori_loop(0, items, drain_side, 0)
 
     mine = part[z]
     for d in range(1, Z):
@@ -299,9 +375,11 @@
                 pltpu.VMEM((Z, ne, spc, LANES), jnp.float32),
                 pltpu.VMEM((max(Z - 1, 1), ne, spc, LANES), jnp.float32),
                 pltpu.VMEM((R, ne, spc, LANES), jnp.float32),
+                pltpu.VMEM((Z, bpd // 2 * states, breadth), jnp.bfloat16),
                 dma((2, 2)), dma, dma((units,)), dma((units,)), dma((units,)),
                 dma((units,)), dma((units,)),
                 dma((Z,)), dma((Z,)), dma((R,)), dma((R,)),
+                dma((Z * bpd,)), dma((Z * bpd,)), dma((Z * bpd * R // Z,)),
             ],
             compiler_params=pltpu.CompilerParams(
                 collective_id=0, has_side_effects=True, vmem_limit_bytes=62 * 1024 * 1024),

time: 181 us -> 172 us (0.950)
  Pallas kernels: 179 us -> 170 us
    pallas_call x1, Pallas kernels: 179 us -> 170 us  [shards(): pl.pallas_call(functools.partial(body, R, Z, bpd, states, height, breadth...]
where the time goes in v2:
time: 172 us; the launch traced here: 171 us
  Pallas kernels  170 us (99%)
    pallas_call x1, Pallas kernels, shards(): pl.pallas_call(functools.partial(body, R, Z, bpd, states, height, breadth...  170 us

profile of v2, /device:TPU:0, one launch (start us, length us, event | category | flops | bytes accessed | tf_op | source)
XLA Modules:
  0.0 171.4 jit_solution(8538399631790866492)
XLA Ops:
  0.0 170.1 %pole_sigma.1 = f32[3,16]{1,0:T(4,128)} custom-call(f32[3]{0:T(128)} %freq.1, f32[32]{0:T(128)} %energy.1, f32[1536,3072]{1,0:T(8,128)} %es_hbm.1, f32[1536,3072]{1,0:T(8,128)} %ei_hbm.1, bf16[256,3072]{1,0:T(8,128)(2,1)} %bitcast.1), custom_call_target="tpu_custom_call" | custom-call | tf_op jit(solution)/shard_map/pole_sigma/pallas_call | solution.py:363
  170.1 1.3 copy.7
